TPU v7x, 32 devices: a whole 2x2x4 slice. The times are simulated.
32 devices in a mesh: dp: 8 (over y, x, core), expert: 4 (over z).
Axes of the slice: x: 2, y: 2, z: 4, core: 2. Of those that a mesh axis runs over, the one named last changes fastest.
Arguments:
- tokens: bfloat16 [512, 2048], P('expert', 'dp'), may hold values from -6 to 6
- routes: int32 [512, 2], P('expert'), may hold values from 0 to 3, all different within a row
- dt_raw: float32 [512, 32], P('expert', 'dp'), may hold values from -5 to 5
- b_proj: float32 [512, 16], P('expert'), may hold values from -1.8 to 1.8
- c_proj: float32 [512, 16], P('expert'), may hold values from -1.8 to 1.8
- decay_rate: float32 [32], P('dp'), may hold values from 0.002 to 0.2
- skip_gain: float32 [32], P('dp'), may hold values from 0.5 to 1.5
- router_weight: float32 [2048, 4], P('dp'), may hold values from -0.125 to 0.125
- gate_weight: bfloat16 [4, 2048, 7168], P('expert', None, 'dp'), may hold values from -0.125 to 0.125
- up_weight: bfloat16 [4, 2048, 7168], P('expert', None, 'dp'), may hold values from -0.125 to 0.125
- down_weight: bfloat16 [4, 7168, 2048], P('expert', 'dp'), may hold values from -0.0625 to 0.0625
- out_grad: bfloat16 [512, 2048], P('expert', 'dp'), may hold values from -6 to 6
Outputs:
- block_out: bfloat16 [512, 2048], P('expert', 'dp')
- token_grad: bfloat16 [512, 2048], P('expert', 'dp')
- gate_grad: bfloat16 [4, 2048, 7168], P('expert', None, 'dp')
- up_grad: bfloat16 [4, 2048, 7168], P('expert', None, 'dp')
- down_grad: bfloat16 [4, 7168, 2048], P('expert', 'dp')
- router_grad: float32 [2048, 4], P('dp')
- rate_grad: float32 [32], P('dp')
- skip_grad: float32 [32], P('dp')
Inputs may be any that keep to these rules, and one draw needn't show every extreme that they name: `routes`: each token names two different experts.
All inputs are finite; a program needn't handle non-finite values.
Results may differ from a plain program's by a relative error of at most 0.02.
Values may be sent and summed in bfloat16 or wider, within the bound.
A program may use at most 64 MiB of HBM per device.

v0:
```python
import jax
import jax.numpy as jnp
from jax import lax
from jax.sharding import PartitionSpec as P

D = 2048
EPSILON = 1e-06
HIGHEST = lax.Precision.HIGHEST


def carried_in(x, axis, combine, identity, reverse):
    peers, place = (lax.axis_size(axis), lax.axis_index(axis))
    everything = jax.tree.map(lambda part: lax.all_gather(part, axis), x)
    start = jax.tree.map(
        lambda part, zero: jnp.broadcast_to(jnp.asarray(zero, part.dtype), part.shape), x, identity
    )

    def lap(k, before):
        at = peers - 1 - k if reverse else k
        reached = at > place if reverse else at < place
        new = combine(before, jax.tree.map(lambda part: part[at], everything))
        return jax.tree.map(lambda a, b: jnp.where(reached, a, b), new, before)

    return lax.fori_loop(0, peers, lap, start)


def end_parts(normed, b_rows, dt_rows, decay_rate):
    steps_total = normed.shape[0]
    head_count = decay_rate.shape[0]
    step_size = jax.nn.softplus(dt_rows)
    running = jnp.cumsum(-step_size * decay_rate[None, :], axis=0)
    tail_weight = jnp.exp(running[-1][None, :] - running) * step_size
    head_rows = normed.reshape(steps_total, head_count, -1)
    local_state = jnp.einsum("sh,shp,sn->hpn", tail_weight, head_rows, b_rows, precision=HIGHEST)
    return (jnp.exp(running[-1]), local_state.reshape(head_count, -1))


def ssd_piece(normed, b_rows, c_rows, dt_rows, decay_rate, skip_gain, state_start):
    steps_total = normed.shape[0]
    head_count = decay_rate.shape[0]
    state_width = b_rows.shape[1]
    step_size = jax.nn.softplus(dt_rows)
    running = jnp.cumsum(-step_size * decay_rate[None, :], axis=0)
    positions = jnp.arange(steps_total, dtype=jnp.int32)
    causal = (positions[:, None] >= positions[None, :])[:, :, None]
    spread = jnp.where(causal, running[:, None, :] - running[None, :, :], 0.0)
    decay_table = jnp.where(causal, jnp.exp(spread), 0.0)
    pairing = jnp.dot(c_rows, b_rows.T, precision=HIGHEST)
    mixing = decay_table * pairing[:, :, None] * step_size[None, :, :]
    head_rows = normed.reshape(steps_total, head_count, -1)
    state_three = state_start.reshape(head_count, -1, state_width)
    mixed = jnp.einsum("tsh,shp->thp", mixing, head_rows, precision=HIGHEST)
    mixed = mixed + jnp.einsum(
        "tn,th,hpn->thp", c_rows, jnp.exp(running), state_three, precision=HIGHEST
    )
    mixed = mixed + skip_gain[None, :, None] * head_rows
    decay_total, local_state = end_parts(normed, b_rows, dt_rows, decay_rate)
    state_end = decay_total[:, None] * state_start + local_state
    return (mixed.reshape(steps_total, -1), state_end)


def dispatch_table(choice_ids, expert_count, capacity):
    flat_ids = choice_ids.reshape(-1)
    row_total = flat_ids.shape[0]
    expert_hot = (flat_ids[:, None] == jnp.arange(expert_count, dtype=jnp.int32)[None, :]).astype(
        jnp.float32
    )
    positions = jnp.arange(row_total, dtype=jnp.int32)
    lower = (positions[:, None] > positions[None, :]).astype(jnp.float32)
    earlier = jnp.dot(lower, expert_hot, precision=HIGHEST)
    slot_index = jnp.sum(earlier * expert_hot, axis=1)
    target = flat_ids.astype(jnp.float32) * capacity + slot_index
    target = jnp.where(slot_index < capacity, target, -1.0)
    slot_ids = jnp.arange(expert_count * capacity, dtype=jnp.int32).astype(jnp.float32)
    return (slot_ids[:, None] == target[None, :]).astype(jnp.float32)


def feature_sum(values):
    return lax.psum(values, "dp")


def norm_scale(values):
    total = feature_sum(jnp.sum(values * values, axis=-1, keepdims=True))
    return lax.rsqrt(total / D + EPSILON)


def norm_back(values, scale, grad):
    inner = feature_sum(jnp.sum(grad * values, axis=-1, keepdims=True))
    return scale * grad - values * (scale * scale * scale) * (inner / D)


def link_states(earlier, later):
    return (earlier[0] * later[0], later[0][:, None] * earlier[1] + later[1])


def carry_states(decay_total, state_part, backward):
    identity = (jnp.ones_like(decay_total), jnp.zeros_like(state_part))
    result = carried_in((decay_total, state_part), "expert", link_states, identity, backward)
    return result[1]


def to_units(send_rows):
    arrived = lax.all_to_all(send_rows, "expert", split_axis=0, concat_axis=0, tiled=True)
    flat_rows = arrived.reshape(-1, arrived.shape[2])
    return lax.all_gather(flat_rows, "dp", axis=1, tiled=True)


def from_units(terms, expert_count):
    summed = lax.psum_scatter(
        terms.astype(jnp.bfloat16), "dp", scatter_dimension=1, tiled=True
    ).astype(jnp.float32)
    shaped = summed.astype(jnp.bfloat16).reshape(expert_count, -1, summed.shape[1])
    returned = lax.all_to_all(shaped, "expert", split_axis=0, concat_axis=0, tiled=True)
    return returned.reshape(-1, summed.shape[1])


def body(
    tokens,
    routes,
    dt_raw,
    b_proj,
    c_proj,
    decay_rate,
    skip_gain,
    router_weight,
    gate_weight,
    up_weight,
    down_weight,
    out_grad,
):
    tok_count = tokens.shape[0]
    feature_count = tokens.shape[1]
    expert_count = lax.axis_size("expert")
    capacity = 5 * tok_count // (2 * expert_count)
    inputs = tokens.astype(jnp.float32)
    scale_one = norm_scale(inputs)
    normed = inputs * scale_one
    decay_total, local_state = end_parts(normed, b_proj, dt_raw, decay_rate)
    state_in = carry_states(decay_total, local_state, False)

    def mixer(normed_in, rate_in, skip_in, state_start):
        return ssd_piece(normed_in, b_proj, c_proj, dt_raw, rate_in, skip_in, state_start)

    (mixed, state_end), mixer_pull = jax.vjp(mixer, normed, decay_rate, skip_gain, state_in)
    resid = (inputs + mixed).astype(jnp.bfloat16)
    resid_f = resid.astype(jnp.float32)
    scale_two = norm_scale(resid_f)
    moe_in = (resid_f * scale_two).astype(jnp.bfloat16)
    moe_f = moe_in.astype(jnp.float32)
    logits = feature_sum(jnp.dot(moe_f, router_weight, precision=HIGHEST))
    expert_ids = jnp.arange(expert_count, dtype=jnp.int32)
    first_hot = (routes[:, 0:1] == expert_ids[None, :]).astype(jnp.float32)
    second_hot = (routes[:, 1:2] == expert_ids[None, :]).astype(jnp.float32)
    logit_gap = jnp.sum(logits * (first_hot - second_hot), axis=1)
    first_weight = jax.nn.sigmoid(logit_gap)
    second_weight = jax.nn.sigmoid(-logit_gap)
    table_b = dispatch_table(routes, expert_count, capacity).astype(jnp.bfloat16)
    doubled = jnp.repeat(moe_in, 2, axis=0)
    send_rows = jnp.dot(table_b, doubled, preferred_element_type=jnp.float32).astype(jnp.bfloat16)
    unit_rows = to_units(send_rows.reshape(expert_count, capacity, feature_count))
    gate_pre = jnp.dot(unit_rows, gate_weight[0], preferred_element_type=jnp.float32)
    up_pre = jnp.dot(unit_rows, up_weight[0], preferred_element_type=jnp.float32)
    hidden = (jax.nn.silu(gate_pre) * up_pre).astype(jnp.bfloat16)
    down_terms = jnp.dot(hidden, down_weight[0], preferred_element_type=jnp.float32)
    back_rows = from_units(down_terms, expert_count)
    per_slot = lax.dot_general(
        table_b, back_rows, (((0,), (0,)), ((), ())), preferred_element_type=jnp.float32
    )
    per_slot = per_slot.reshape(tok_count, 2, feature_count)
    moe_sum = first_weight[:, None] * per_slot[:, 0] + second_weight[:, None] * per_slot[:, 1]
    block_out = (resid_f + moe_sum).astype(jnp.bfloat16)
    upstream = out_grad.astype(jnp.float32)
    back_pair = feature_sum(jnp.sum(upstream[:, None, :] * per_slot, axis=2))
    first_back = back_pair[:, 0]
    second_back = back_pair[:, 1]
    slot_grad = jnp.stack(
        [first_weight[:, None] * upstream, second_weight[:, None] * upstream], axis=1
    )
    slot_grad = slot_grad.reshape(2 * tok_count, feature_count).astype(jnp.bfloat16)
    grad_send = jnp.dot(table_b, slot_grad, preferred_element_type=jnp.float32).astype(jnp.bfloat16)
    grad_rows = to_units(grad_send.reshape(expert_count, capacity, feature_count))
    unit_grad = lax.dot_general(
        grad_rows, down_weight[0], (((1,), (1,)), ((), ())), preferred_element_type=jnp.float32
    )
    sigma = jax.nn.sigmoid(gate_pre)
    gate_back = (unit_grad * up_pre * sigma * (1.0 + gate_pre * (1.0 - sigma))).astype(jnp.bfloat16)
    up_back = (unit_grad * jax.nn.silu(gate_pre)).astype(jnp.bfloat16)
    down_part = lax.dot_general(
        hidden, grad_rows, (((0,), (0,)), ((), ())), preferred_element_type=jnp.float32
    )
    gate_part = lax.dot_general(
        unit_rows, gate_back, (((0,), (0,)), ((), ())), preferred_element_type=jnp.float32
    )
    up_part = lax.dot_general(
        unit_rows, up_back, (((0,), (0,)), ((), ())), preferred_element_type=jnp.float32
    )
    gate_done = gate_part.astype(jnp.bfloat16)
    up_done = up_part.astype(jnp.bfloat16)
    down_done = down_part.astype(jnp.bfloat16)
    gate_side = lax.dot_general(
        gate_back, gate_weight[0], (((1,), (1,)), ((), ())), preferred_element_type=jnp.float32
    )
    up_side = lax.dot_general(
        up_back, up_weight[0], (((1,), (1,)), ((), ())), preferred_element_type=jnp.float32
    )
    returned = from_units(gate_side + up_side, expert_count)
    slot_back = lax.dot_general(
        table_b, returned, (((0,), (0,)), ((), ())), preferred_element_type=jnp.float32
    )
    slot_back = slot_back.reshape(tok_count, 2, feature_count)
    moe_grad = slot_back[:, 0] + slot_back[:, 1]
    gap_grad = first_weight * second_weight * (first_back - second_back)
    logit_grad = gap_grad[:, None] * (first_hot - second_hot)
    moe_in_grad = moe_grad + jnp.dot(logit_grad, router_weight.T, precision=HIGHEST)
    router_part = jnp.dot(moe_f.T, logit_grad, precision=HIGHEST)
    resid_grad = upstream + norm_back(resid_f, scale_two, moe_in_grad)
    zero_state = jnp.zeros_like(state_end)
    local_pull = mixer_pull((resid_grad, zero_state))
    later_grad = carry_states(decay_total, local_pull[3], True)
    tail_pull = mixer_pull((jnp.zeros_like(resid_grad), later_grad))
    normed_grad = local_pull[0] + tail_pull[0]
    rate_part = local_pull[1] + tail_pull[1]
    skip_part = local_pull[2] + tail_pull[2]
    token_grad = (resid_grad + norm_back(inputs, scale_one, normed_grad)).astype(jnp.bfloat16)
    router_total, rate_total, skip_total = lax.psum((router_part, rate_part, skip_part), "expert")
    return (
        block_out,
        token_grad,
        gate_done[None],
        up_done[None],
        down_done[None],
        router_total,
        rate_total,
        skip_total,
    )


def solution(mesh):
    return jax.shard_map(
        body,
        mesh=mesh,
        in_specs=(
            P("expert", "dp"),
            P("expert", None),
            P("expert", "dp"),
            P("expert", None),
            P("expert", None),
            P("dp"),
            P("dp"),
            P("dp", None),
            P("expert", None, "dp"),
            P("expert", None, "dp"),
            P("expert", "dp", None),
            P("expert", "dp"),
        ),
        out_specs=(
            P("expert", "dp"),
            P("expert", "dp"),
            P("expert", None, "dp"),
            P("expert", None, "dp"),
            P("expert", "dp", None),
            P("dp", None),
            P("dp"),
            P("dp"),
        ),
        check_vma=False,
    )
```

profile of v0, /device:TPU:0, one launch (start us, length us, event | category | flops | bytes accessed | tf_op | source)
XLA Modules:
  0.0 330.2 jit_solution(9613662080499625949)
XLA Ops:
  9.4 15.2 %psum.63 = f32[128,1]{0,1:T(1,128)S(1)} all-reduce(f32[128,1]{0,1:T(1,128)S(1)} %bitcast.271), channel_id=1, replica_groups=mesh['dp'=8,'expert'=4] {'dp'}, use_global_device_ids=true, to_apply=%region_1.0 | all-reduce | flops 128 | bytes 1024 | tf_op jit(solution)/shard_map/psum | solution.py:79
  24.8 11.2 %all-gather = f32[4,1,4]{2,1,0:T(1,128)S(1)} all-gather(f32[1,1,4]{2,1,0:T(1,128)S(1)} %bitcast.267), channel_id=1, replica_groups=mesh['dp'=8,'expert'=4] {'expert'}, dimensions={0}, use_global_device_ids=true | all-gather | bytes 80 | tf_op jit(solution)/shard_map/all_gather | solution.py:13
  40.3 13.1 %all_gather.20 = f32[4,4,1024]{2,1,0:T(4,128)S(1)} all-gather(f32[1,4,1024]{2,1,0:T(4,128)S(1)} %all_gather_reshape.3), channel_id=1, replica_groups=mesh['dp'=8,'expert'=4] {'expert'}, dimensions={0}, use_global_device_ids=true | all-gather | bytes 81920 | tf_op jit(solution)/shard_map/all_gather | solution.py:13
  55.1 11.8 %psum.64 = f32[128,1]{0,1:T(1,128)S(1)} all-reduce(f32[128,1]{0,1:T(1,128)S(1)} %bitcast.269), channel_id=1, replica_groups=mesh['dp'=8,'expert'=4] {'dp'}, use_global_device_ids=true, to_apply=%region_6.7 | all-reduce | flops 128 | bytes 1024 | tf_op jit(solution)/shard_map/psum | solution.py:79
  67.4 10.0 %all_to_all.20 = bf16[4,80,256]{2,1,0:T(8,128)(2,1)} all-to-all(bf16[4,80,256]{2,1,0:T(8,128)(2,1)S(1)} %bitcast.259), channel_id=1, replica_groups=mesh['dp'=8,'expert'=4] {'expert'}, dimensions={0} | all-to-all | bytes 327680 | tf_op jit(solution)/shard_map/all_to_all | solution.py:103
  77.6 22.0 %all-gather.4.cloned.1.call-done = bf16[320,2048]{1,0:T(8,128)(2,1)} async-done(((bf16[320,256]{1,0:T(8,128)(2,1)}), bf16[320,2048]{1,0:T(8,128)(2,1)}) %all-gather.4.cloned.1.call-update) | async-done | bytes 1310736 | tf_op jit(solution)/shard_map/all_gather | solution.py:105
  99.6 4.1 %fusion.12 = f32[320,896]{1,0:T(8,128)S(1)} fusion(bf16[320,2048]{1,0:T(8,128)(2,1)} %all-gather.4.cloned.1.call-done, bf16[1,2048,896]{2,1,0:T(8,128)(2,1)} %param.24), kind=kOutput, calls=%fused_computation.16 | convolution fusion | flops 1174405120 | bytes 6127616 | tf_op jit(solution)/shard_map/dot_general | solution.py:161
  107.2 2.6 fusion.20
  110.6 36.6 %reduce-scatter.3.cloned.1.call-done = bf16[320,256]{1,0:T(8,128)(2,1)} async-done(((bf16[320,2048]{1,0:T(8,128)(2,1)}), bf16[320,256]{1,0:T(8,128)(2,1)}) %reduce-scatter.3.cloned.1.call-update) | async-done | bytes 163856 | tf_op jit(solution)/shard_map/reduce_scatter | solution.py:109
  147.2 4.6 %all-to-all-start.1 = ((bf16[4,80,256]{2,1,0:T(8,128)(2,1)}), bf16[4,80,256]{2,1,0:T(8,128)(2,1)S(1)}, u32[]{:S(2)}, u32[]{:S(2)}) async-start(bf16[4,80,256]{2,1,0:T(8,128)(2,1)} %bitcast.257), calls=%async_computation.2 | async-start | bytes 327680 | tf_op jit(solution)/shard_map/all_to_all | solution.py:113
  152.0 6.2 %all-to-all-done.1 = bf16[4,80,256]{2,1,0:T(8,128)(2,1)S(1)} async-done(((bf16[4,80,256]{2,1,0:T(8,128)(2,1)}), bf16[4,80,256]{2,1,0:T(8,128)(2,1)S(1)}, u32[]{:S(2)}, u32[]{:S(2)}) %all-to-all-start.1) | async-done | bytes 163872 | tf_op jit(solution)/shard_map/all_to_all | solution.py:113
  158.6 11.8 %all-reduce.4 = (f32[128,4]{0,1:T(4,128)S(1)}, f32[128,2]{0,1:T(2,128)S(1)}) all-reduce(f32[128,4]{0,1:T(4,128)S(1)} %fusion.157, f32[128,2]{0,1:T(2,128)S(1)} %get-tuple-element.343), channel_id=1, replica_groups=mesh['dp'=8,'expert'=4] {'dp'}, use_global_device_ids=true, to_apply=%region_7.8 | all-reduce | flops 768 | bytes 6144 | tf_op jit(solution)/shard_map/psum | solution.py:79
  171.1 10.0 %all_to_all.21 = bf16[4,80,256]{2,1,0:T(8,128)(2,1)} all-to-all(bf16[4,80,256]{2,1,0:T(8,128)(2,1)S(1)} %bitcast.258), channel_id=1, replica_groups=mesh['dp'=8,'expert'=4] {'expert'}, dimensions={0} | all-to-all | bytes 327680 | tf_op jit(solution)/shard_map/all_to_all | solution.py:103
  181.4 22.7 %all-gather.6.cloned.1.call-done = bf16[320,2048]{1,0:T(8,128)(2,1)} async-done(((bf16[320,256]{1,0:T(8,128)(2,1)}), bf16[320,2048]{1,0:T(8,128)(2,1)}) %all-gather.6.cloned.1.call-update) | async-done | bytes 1310736 | tf_op jit(solution)/shard_map/all_gather | solution.py:105
  204.1 5.0 %multiply_convert_fusion.1 = (bf16[320,896]{1,0:T(8,128)(2,1)S(1)}, bf16[320,896]{1,0:T(8,128)(2,1)S(1)}) fusion(f32[320,896]{1,0:T(8,128)} %copy-done.13, f32[320,896]{1,0:T(8,128)} %get-tuple-element.342, bf16[320,2048]{1,0:T(8,128)(2,1)} %all-gather.6.cloned.1.call-done, bf16[1,896,2048]{2,1,0:T(8,128)(2,1)} %param.26), kind=kOutput, calls=%fused_computation.39 | convolution fusion | flops 1178132480 | bytes 8421376 | tf_op jit(solution)/shard_map/dot_general | solution.py:182
  215.7 5.5 %convert_bitcast_fusion = bf16[1,896,2048]{2,1,0:T(8,128)(2,1)} fusion(bf16[320,896]{1,0:T(8,128)(2,1)} %copy-done.14, bf16[320,2048]{1,0:T(8,128)(2,1)} %all-gather.6.cloned.1.call-done), kind=kOutput, calls=%fused_computation.18 | convolution fusion | flops 1176240128 | bytes 5554176 | tf_op jit(solution)/shard_map/dot_general | solution.py:188
  221.3 4.1 %convert_bitcast_fusion.2 = bf16[1,2048,896]{2,1,0:T(8,128)(2,1)} fusion(bf16[320,2048]{1,0:T(8,128)(2,1)S(1)} %copy-done.11, bf16[320,896]{1,0:T(8,128)(2,1)S(1)} %copy-done.16), kind=kOutput, calls=%fused_computation.20 | convolution fusion | flops 1176240128 | bytes 5554176 | tf_op jit(solution)/shard_map/dot_general | solution.py:191
  225.4 26.0 %reduce-scatter.5.cloned.1.call-done = bf16[320,256]{1,0:T(8,128)(2,1)} async-done(((bf16[320,2048]{1,0:T(8,128)(2,1)}), bf16[320,256]{1,0:T(8,128)(2,1)}) %reduce-scatter.5.cloned.1.call-update) | async-done | bytes 163856 | tf_op jit(solution)/shard_map/reduce_scatter | solution.py:109
  251.4 4.6 %all-to-all-start.3 = ((bf16[4,80,256]{2,1,0:T(8,128)(2,1)}), bf16[4,80,256]{2,1,0:T(8,128)(2,1)S(1)}, u32[]{:S(2)}, u32[]{:S(2)}) async-start(bf16[4,80,256]{2,1,0:T(8,128)(2,1)} %bitcast.256), calls=%async_computation.5 | async-start | bytes 327680 | tf_op jit(solution)/shard_map/all_to_all | solution.py:113
  256.0 4.1 %convert_bitcast_fusion.1 = bf16[1,2048,896]{2,1,0:T(8,128)(2,1)} fusion(bf16[320,2048]{1,0:T(8,128)(2,1)S(1)} %copy-done.11, bf16[320,896]{1,0:T(8,128)(2,1)S(1)} %get-tuple-element.322), kind=kOutput, calls=%fused_computation.19 | convolution fusion | flops 1176240128 | bytes 5554176 | tf_op jit(solution)/shard_map/dot_general | solution.py:194
  263.2 12.0 %psum.67 = f32[128,1]{0,1:T(1,128)S(1)} all-reduce(f32[128,1]{0,1:T(1,128)S(1)} %bitcast.268), channel_id=1, replica_groups=mesh['dp'=8,'expert'=4] {'dp'}, use_global_device_ids=true, to_apply=%region_15.16 | all-reduce | flops 128 | bytes 1024 | tf_op jit(solution)/shard_map/psum | solution.py:79
  276.9 13.1 %all_gather.23 = f32[4,4,1024]{2,1,0:T(4,128)S(1)} all-gather(f32[1,4,1024]{2,1,0:T(4,128)S(1)} %broadcast_add_fusion), channel_id=1, replica_groups=mesh['dp'=8,'expert'=4] {'expert'}, dimensions={0}, use_global_device_ids=true | all-gather | bytes 81920 | tf_op jit(solution)/shard_map/all_gather | solution.py:13
  296.9 11.8 %psum.68 = f32[128,1]{0,1:T(1,128)S(1)} all-reduce(f32[128,1]{0,1:T(1,128)S(1)} %bitcast.270), channel_id=1, replica_groups=mesh['dp'=8,'expert'=4] {'dp'}, use_global_device_ids=true, to_apply=%region_19.20 | all-reduce | flops 128 | bytes 1024 | tf_op jit(solution)/shard_map/psum | solution.py:79
  312.8 10.8 %all-reduce.5 = (f32[256,4]{0,1:T(4,128)}, f32[4]{0:T(128)}, f32[4]{0:T(128)}) all-reduce(f32[256,4]{0,1:T(4,128)S(1)} %fusion.126, f32[4]{0:T(128)S(1)} %add_add_fusion, f32[4]{0:T(128)S(1)} %add.227), channel_id=1, replica_groups=mesh['dp'=8,'expert'=4] {'expert'}, use_global_device_ids=true, to_apply=%region_20.21 | all-reduce | flops 1032 | bytes 8256 | tf_op jit(solution)/shard_map/psum | solution.py:225
  (175 shorter events, 37.5 us)
Async XLA Ops:
  7.2 144.7 %copy-start = (f32[256,4]{0,1:T(4,128)S(1)}, f32[256,4]{0,1:T(4,128)}, u32[]{:S(2)}) copy-start(f32[256,4]{0,1:T(4,128)} %param.23) | copy-start | bytes 12292
  7.2 32.8 %copy-start.3 = (f32[128,16]{0,1:T(8,128)S(1)}, f32[128,16]{0,1:T(8,128)}, u32[]{:S(2)}) copy-start(f32[128,16]{0,1:T(8,128)} %param.19) | copy-start | bytes 24580
  7.2 46.7 %copy-start.4 = (f32[128,16]{0,1:T(8,128)S(1)}, f32[128,16]{0,1:T(8,128)}, u32[]{:S(2)}) copy-start(f32[128,16]{0,1:T(8,128)} %param.20) | copy-start | bytes 24580
  7.2 92.4 %all-gather.4.cloned.1.call-start = ((), (), s32[]{:S(2)}) async-start(), calls=%async_computation.6 | async-start | bytes 1474560 | tf_op jit(solution)/shard_map/all_gather | solution.py:105
  8.2 46.0 %copy-start.12 = (f32[4]{0:T(128)S(1)}, f32[4]{0:T(128)}, u32[]{:S(2)}) copy-start(f32[4]{0:T(128)} %param.22) | copy-start | bytes 52
  38.8 16.2 %copy-start.1 = (bf16[128,256]{1,0:T(8,128)(2,1)S(1)}, bf16[128,256]{1,0:T(8,128)(2,1)}, u32[]{:S(2)}) copy-start(bf16[128,256]{1,0:T(8,128)(2,1)} %param.16) | copy-start | bytes 196612
  77.5 69.7 %reduce-scatter.3.cloned.1.call-start = ((), (), s32[]{:S(2)}) async-start(), calls=%async_computation.7 | async-start | bytes 1474560 | tf_op jit(solution)/shard_map/reduce_scatter | solution.py:109
  99.6 4.1 %copy-start.8 = (bf16[1,2048,896]{2,1,0:T(8,128)(2,1)S(1)}, bf16[1,2048,896]{2,1,0:T(8,128)(2,1)}, u32[]{:S(2)}) copy-start(bf16[1,2048,896]{2,1,0:T(8,128)(2,1)} %param.25) | copy-start | bytes 11010052
  99.6 4.1 %copy-start.11 = (bf16[320,2048]{1,0:T(8,128)(2,1)S(1)}, bf16[320,2048]{1,0:T(8,128)(2,1)}, u32[]{:S(2)}) copy-start(bf16[320,2048]{1,0:T(8,128)(2,1)} %all-gather.4.cloned.1.call-done) | copy-start | bytes 3932164
  103.7 2.6 copy-start.13
  103.7 3.5 %copy-start.7 = (bf16[1,896,2048]{2,1,0:T(8,128)(2,1)S(1)}, bf16[1,896,2048]{2,1,0:T(8,128)(2,1)}, u32[]{:S(2)}) copy-start(bf16[1,896,2048]{2,1,0:T(8,128)(2,1)} %param.26) | copy-start | bytes 11010052
  106.3 0.8 copy-start.14
  109.8 0.7 copy-start.6
  109.8 42.0 %copy-start.2 = (bf16[128,256]{1,0:T(8,128)(2,1)S(1)}, bf16[128,256]{1,0:T(8,128)(2,1)}, u32[]{:S(2)}) copy-start(bf16[128,256]{1,0:T(8,128)(2,1)} %param.27) | copy-start | bytes 196612
  147.2 11.0 %all-to-all-start.1 = ((bf16[4,80,256]{2,1,0:T(8,128)(2,1)}), bf16[4,80,256]{2,1,0:T(8,128)(2,1)S(1)}, u32[]{:S(2)}, u32[]{:S(2)}) async-start(bf16[4,80,256]{2,1,0:T(8,128)(2,1)} %bitcast.257), calls=%async_computation.2 | async-start | bytes 327680 | tf_op jit(solution)/shard_map/all_to_all | solution.py:113
  151.8 52.3 %all-gather.6.cloned.1.call-start = ((), (), s32[]{:S(2)}) async-start(), calls=%async_computation.8 | async-start | bytes 1474560 | tf_op jit(solution)/shard_map/all_gather | solution.py:105
  181.1 70.2 %reduce-scatter.5.cloned.1.call-start = ((), (), s32[]{:S(2)}) async-start(), calls=%async_computation.9 | async-start | bytes 1474560 | tf_op jit(solution)/shard_map/reduce_scatter | solution.py:109
  204.1 5.0 %copy-start.9 = (bf16[1,2048,896]{2,1,0:T(8,128)(2,1)S(1)}, bf16[1,2048,896]{2,1,0:T(8,128)(2,1)}, u32[]{:S(2)}) copy-start(bf16[1,2048,896]{2,1,0:T(8,128)(2,1)} %param.25) | copy-start | bytes 11010052
  209.1 1.6 copy-start.15
  209.1 2.2 copy-start.10
  215.7 5.5 %copy-start.16 = (bf16[320,896]{1,0:T(8,128)(2,1)S(1)}, bf16[320,896]{1,0:T(8,128)(2,1)}, u32[]{:S(2)}) copy-start(bf16[320,896]{1,0:T(8,128)(2,1)} %copy-done.15) | copy-start | bytes 1720324
  251.4 11.0 %all-to-all-start.3 = ((bf16[4,80,256]{2,1,0:T(8,128)(2,1)}), bf16[4,80,256]{2,1,0:T(8,128)(2,1)S(1)}, u32[]{:S(2)}, u32[]{:S(2)}) async-start(bf16[4,80,256]{2,1,0:T(8,128)(2,1)} %bitcast.256), calls=%async_computation.5 | async-start | bytes 327680 | tf_op jit(solution)/shard_map/all_to_all | solution.py:113
  292.2 4.1 %copy-start.5 = (f32[128,4]{0,1:T(4,128)S(1)}, f32[128,4]{0,1:T(4,128)}, u32[]{:S(2)}) copy-start(f32[128,4]{0,1:T(4,128)} %param.18) | copy-start | bytes 6148
Sparse Core Ops, SparseCore 0:
  77.6 21.9 all-gather.3
  109.9 37.1 reduce-scatter.2
  181.2 22.7 all-gather.5
  214.1 37.1 reduce-scatter.4
where the time goes:
time: 331 us; the launch traced here: 330 us
  blocking collectives  131 us (40%)
  waiting for transfers between devices  116 us (35%)
  matrix products  40.8 us (12%)
  between operations  14.3 us (4%)
  other arithmetic  11.9 us (4%)
  starting transfers between devices  9.5 us (3%)
  local copies, waits for them, and re-layouts  6.81 us (2%)
    psum x5, blocking collectives, feature_sum(): return lax.psum(values, 'dp')  62.6 us
    reduce_scatter x2, waiting for transfers between devices, from_units(): lax.psum_scatter(terms.astype(jnp.bfloat16), 'dp', scatter_dimension=1, t...  62.5 us
    all_gather x2, waiting for transfers between devices, to_units(): return lax.all_gather(flat_rows, 'dp', axis=1, tiled=True)  44.8 us
    all_gather x3, blocking collectives, carried_in(): everything = jax.tree.map(lambda part: lax.all_gather(part, axis), x)  37.4 us
    all_to_all x2, blocking collectives, to_units(): lax.all_to_all(send_rows, 'expert', split_axis=0, concat_axis=0, tiled=True)  20.1 us
    psum x1, blocking collectives, body(): lax.psum((router_part, rate_part, skip_part), 'expert')  10.8 us
    all_to_all x2, starting transfers between devices, from_units(): lax.all_to_all(shaped, 'expert', split_axis=0, concat_axis=0, tiled=True)  9.2 us
    all_to_all x2, waiting for transfers between devices, from_units(): lax.all_to_all(shaped, 'expert', split_axis=0, concat_axis=0, tiled=True)  8.5 us
  transfers between devices with their start and end apart: 6, of which 6 were waited for; matrix products, arithmetic and copies ran while one was open for 5% of the time, Pallas kernels for 0%

commit v1 on v0

--- a/solution.py
+++ b/solution.py
@@ -76,7 +76,7 @@
 
 
 def feature_sum(values):
-    return lax.psum(values, "dp")
+    return jnp.sum(lax.all_gather(values, "dp"), axis=0)
 
 
 def norm_scale(values):

time: 331 us -> 318 us (0.961)
  blocking collectives: 131 us -> 123 us
  waiting for transfers between devices: 116 us -> 110 us
    psum x5 -> x0, blocking collectives: 62.6 us -> none  [feature_sum(): return lax.psum(values, 'dp')]
    all_gather x0 -> x6, blocking collectives: none -> 52.7 us  [feature_sum(): return jnp.sum(lax.all_gather(values, 'dp'), axis=0)]
    all_to_all x2, waiting for transfers between devices: 8.5 us -> 2.31 us  [from_units(): lax.all_to_all(shaped, 'expert', split_axis=0, concat_axis=0, tiled=True)]
  transfers between devices with their start and end apart: 6 -> 6, of which waited for: 6 -> 5; matrix products, arithmetic and copies ran while one was open for 5% -> 5% of each run, Pallas kernels for 0% -> 0%
where the time goes in v1:
time: 318 us; the launch traced here: 317 us
  blocking collectives  123 us (39%)
  waiting for transfers between devices  110 us (35%)
  matrix products  40.8 us (13%)
  between operations  14.3 us (4%)
  other arithmetic  12.1 us (4%)
  starting transfers between devices  9.5 us (3%)
  local copies, waits for them, and re-layouts  6.85 us (2%)
    reduce_scatter x2, waiting for transfers between devices, from_units(): lax.psum_scatter(terms.astype(jnp.bfloat16), 'dp', scatter_dimension=1, t...  62.4 us
    all_gather x6, blocking collectives, feature_sum(): return jnp.sum(lax.all_gather(values, 'dp'), axis=0)  52.7 us
    all_gather x2, waiting for transfers between devices, to_units(): return lax.all_gather(flat_rows, 'dp', axis=1, tiled=True)  45.7 us
    all_gather x3, blocking collectives, carried_in(): everything = jax.tree.map(lambda part: lax.all_gather(part, axis), x)  37.4 us
    all_to_all x2, blocking collectives, to_units(): lax.all_to_all(send_rows, 'expert', split_axis=0, concat_axis=0, tiled=True)  22.7 us
    psum x1, blocking collectives, body(): lax.psum((router_part, rate_part, skip_part), 'expert')  10.6 us
    all_to_all x2, starting transfers between devices, from_units(): lax.all_to_all(shaped, 'expert', split_axis=0, concat_axis=0, tiled=True)  9.2 us
  transfers between devices with their start and end apart: 6, of which 5 were waited for; matrix products, arithmetic and copies ran while one was open for 5% of the time, Pallas kernels for 0%

profile of v1, /device:TPU:0, one launch (start us, length us, event | category | flops | bytes accessed | tf_op | source)
XLA Modules:
  0.0 317.5 jit_solution(10537946823368863085)
XLA Ops:
  9.4 10.3 %all-gather.6 = f32[8,1,128]{2,1,0:T(1,128)S(1)} all-gather(f32[1,1,128]{2,1,0:T(1,128)S(1)} %bitcast.267), channel_id=2, replica_groups=mesh['dp'=8,'expert'=4] {'dp'}, dimensions={0}, use_global_device_ids=true | all-gather | bytes 4608 | tf_op jit(solution)/shard_map/all_gather | solution.py:79
  19.9 11.2 %all-gather.7 = f32[4,1,4]{2,1,0:T(1,128)S(1)} all-gather(f32[1,1,4]{2,1,0:T(1,128)S(1)} %bitcast.271), channel_id=1, replica_groups=mesh['dp'=8,'expert'=4] {'expert'}, dimensions={0}, use_global_device_ids=true | all-gather | bytes 80 | tf_op jit(solution)/shard_map/all_gather | solution.py:13
  35.5 13.1 %all_gather.45 = f32[4,4,1024]{2,1,0:T(4,128)S(1)} all-gather(f32[1,4,1024]{2,1,0:T(4,128)S(1)} %all_gather_reshape.3), channel_id=1, replica_groups=mesh['dp'=8,'expert'=4] {'expert'}, dimensions={0}, use_global_device_ids=true | all-gather | bytes 81920 | tf_op jit(solution)/shard_map/all_gather | solution.py:13
  50.3 8.8 %all-gather.8 = f32[8,1,128]{2,1,0:T(1,128)S(1)} all-gather(f32[1,1,128]{2,1,0:T(1,128)S(1)} %bitcast.266), channel_id=3, replica_groups=mesh['dp'=8,'expert'=4] {'dp'}, dimensions={0}, use_global_device_ids=true | all-gather | bytes 4608 | tf_op jit(solution)/shard_map/all_gather | solution.py:79
  59.6 10.5 %all_to_all.20 = bf16[4,80,256]{2,1,0:T(8,128)(2,1)} all-to-all(bf16[4,80,256]{2,1,0:T(8,128)(2,1)S(1)} %bitcast.257), channel_id=1, replica_groups=mesh['dp'=8,'expert'=4] {'expert'}, dimensions={0} | all-to-all | bytes 327680 | tf_op jit(solution)/shard_map/all_to_all | solution.py:103
  70.2 22.9 %all-gather.14.cloned.1.call-done = bf16[320,2048]{1,0:T(8,128)(2,1)} async-done(((bf16[320,256]{1,0:T(8,128)(2,1)}), bf16[320,2048]{1,0:T(8,128)(2,1)}) %all-gather.14.cloned.1.call-update) | async-done | bytes 1310736 | tf_op jit(solution)/shard_map/all_gather | solution.py:105
  93.1 4.1 %fusion.12 = f32[320,896]{1,0:T(8,128)S(1)} fusion(bf16[320,2048]{1,0:T(8,128)(2,1)} %all-gather.14.cloned.1.call-done, bf16[1,2048,896]{2,1,0:T(8,128)(2,1)} %param.24), kind=kOutput, calls=%fused_computation.16 | convolution fusion | flops 1174405120 | bytes 6127616 | tf_op jit(solution)/shard_map/dot_general | solution.py:161
  100.7 2.6 fusion.20
  104.3 36.4 %reduce-scatter.3.cloned.1.call-done = bf16[320,256]{1,0:T(8,128)(2,1)} async-done(((bf16[320,2048]{1,0:T(8,128)(2,1)}), bf16[320,256]{1,0:T(8,128)(2,1)}) %reduce-scatter.3.cloned.1.call-update) | async-done | bytes 163856 | tf_op jit(solution)/shard_map/reduce_scatter | solution.py:109
  140.7 4.6 %all-to-all-start.1 = ((bf16[4,80,256]{2,1,0:T(8,128)(2,1)}), bf16[4,80,256]{2,1,0:T(8,128)(2,1)S(1)}, u32[]{:S(2)}, u32[]{:S(2)}) async-start(bf16[4,80,256]{2,1,0:T(8,128)(2,1)} %bitcast.255), calls=%async_computation.2 | async-start | bytes 327680 | tf_op jit(solution)/shard_map/all_to_all | solution.py:113
  145.4 8.9 %all-gather.2 = f32[1024,4]{0,1:T(4,128)S(1)} all-gather(f32[128,4]{0,1:T(4,128)S(1)} %fusion.153), channel_id=4, replica_groups=mesh['dp'=8,'expert'=4] {'dp'}, dimensions={0}, use_global_device_ids=true | all-gather | bytes 18432 | tf_op jit(solution)/shard_map/all_gather | solution.py:79
  154.7 8.0 %all-gather.3 = f32[1024,2]{0,1:T(2,128)S(1)} all-gather(f32[128,2]{0,1:T(2,128)S(1)} %get-tuple-element.341), channel_id=5, replica_groups=mesh['dp'=8,'expert'=4] {'dp'}, dimensions={0}, use_global_device_ids=true | all-gather | bytes 9216 | tf_op jit(solution)/shard_map/all_gather | solution.py:79
  163.4 12.2 %all_to_all.21 = bf16[4,80,256]{2,1,0:T(8,128)(2,1)} all-to-all(bf16[4,80,256]{2,1,0:T(8,128)(2,1)S(1)} %bitcast.256), channel_id=1, replica_groups=mesh['dp'=8,'expert'=4] {'expert'}, dimensions={0} | all-to-all | bytes 327680 | tf_op jit(solution)/shard_map/all_to_all | solution.py:103
  175.8 22.7 %all-gather.16.cloned.1.call-done = bf16[320,2048]{1,0:T(8,128)(2,1)} async-done(((bf16[320,256]{1,0:T(8,128)(2,1)}), bf16[320,2048]{1,0:T(8,128)(2,1)}) %all-gather.16.cloned.1.call-update) | async-done | bytes 1310736 | tf_op jit(solution)/shard_map/all_gather | solution.py:105
  198.6 5.0 %multiply_convert_fusion.1 = (bf16[320,896]{1,0:T(8,128)(2,1)S(1)}, bf16[320,896]{1,0:T(8,128)(2,1)S(1)}) fusion(f32[320,896]{1,0:T(8,128)} %copy-done.13, f32[320,896]{1,0:T(8,128)} %get-tuple-element.340, bf16[320,2048]{1,0:T(8,128)(2,1)} %all-gather.16.cloned.1.call-done, bf16[1,896,2048]{2,1,0:T(8,128)(2,1)} %param.26), kind=kOutput, calls=%fused_computation.39 | convolution fusion | flops 1178132480 | bytes 8421376 | tf_op jit(solution)/shard_map/dot_general | solution.py:182
  210.2 5.5 %convert_bitcast_fusion = bf16[1,896,2048]{2,1,0:T(8,128)(2,1)} fusion(bf16[320,896]{1,0:T(8,128)(2,1)} %copy-done.14, bf16[320,2048]{1,0:T(8,128)(2,1)} %all-gather.16.cloned.1.call-done), kind=kOutput, calls=%fused_computation.18 | convolution fusion | flops 1176240128 | bytes 5554176 | tf_op jit(solution)/shard_map/dot_general | solution.py:188
  215.7 4.1 %convert_bitcast_fusion.2 = bf16[1,2048,896]{2,1,0:T(8,128)(2,1)} fusion(bf16[320,2048]{1,0:T(8,128)(2,1)S(1)} %copy-done.11, bf16[320,896]{1,0:T(8,128)(2,1)S(1)} %copy-done.16), kind=kOutput, calls=%fused_computation.20 | convolution fusion | flops 1176240128 | bytes 5554176 | tf_op jit(solution)/shard_map/dot_general | solution.py:191
  219.8 26.0 %reduce-scatter.5.cloned.1.call-done = bf16[320,256]{1,0:T(8,128)(2,1)} async-done(((bf16[320,2048]{1,0:T(8,128)(2,1)}), bf16[320,256]{1,0:T(8,128)(2,1)}) %reduce-scatter.5.cloned.1.call-update) | async-done | bytes 163856 | tf_op jit(solution)/shard_map/reduce_scatter | solution.py:109
  245.8 4.6 %all-to-all-start.3 = ((bf16[4,80,256]{2,1,0:T(8,128)(2,1)}), bf16[4,80,256]{2,1,0:T(8,128)(2,1)S(1)}, u32[]{:S(2)}, u32[]{:S(2)}) async-start(bf16[4,80,256]{2,1,0:T(8,128)(2,1)} %bitcast.254), calls=%async_computation.5 | async-start | bytes 327680 | tf_op jit(solution)/shard_map/all_to_all | solution.py:113
  250.4 4.1 %convert_bitcast_fusion.1 = bf16[1,2048,896]{2,1,0:T(8,128)(2,1)} fusion(bf16[320,2048]{1,0:T(8,128)(2,1)S(1)} %copy-done.11, bf16[320,896]{1,0:T(8,128)(2,1)S(1)} %get-tuple-element.320), kind=kOutput, calls=%fused_computation.19 | convolution fusion | flops 1176240128 | bytes 5554176 | tf_op jit(solution)/shard_map/dot_general | solution.py:194
  257.6 9.0 %all-gather.9 = f32[8,1,128]{2,1,0:T(1,128)S(1)} all-gather(f32[1,1,128]{2,1,0:T(1,128)S(1)} %bitcast.265), channel_id=6, replica_groups=mesh['dp'=8,'expert'=4] {'dp'}, dimensions={0}, use_global_device_ids=true | all-gather | bytes 4608 | tf_op jit(solution)/shard_map/all_gather | solution.py:79
  268.3 13.1 %all_gather.54 = f32[4,4,1024]{2,1,0:T(4,128)S(1)} all-gather(f32[1,4,1024]{2,1,0:T(4,128)S(1)} %broadcast_add_fusion), channel_id=1, replica_groups=mesh['dp'=8,'expert'=4] {'expert'}, dimensions={0}, use_global_device_ids=true | all-gather | bytes 81920 | tf_op jit(solution)/shard_map/all_gather | solution.py:13
  288.7 7.8 %all-gather.10 = f32[8,1,128]{2,1,0:T(1,128)S(1)} all-gather(f32[1,1,128]{2,1,0:T(1,128)S(1)} %bitcast.264), channel_id=7, replica_groups=mesh['dp'=8,'expert'=4] {'dp'}, dimensions={0}, use_global_device_ids=true | all-gather | bytes 4608 | tf_op jit(solution)/shard_map/all_gather | solution.py:79
  300.3 10.6 %all-reduce.4 = (f32[256,4]{0,1:T(4,128)}, f32[4]{0:T(128)}, f32[4]{0:T(128)}) all-reduce(f32[256,4]{0,1:T(4,128)S(1)} %fusion.126, f32[4]{0:T(128)S(1)} %add_add_fusion, f32[4]{0:T(128)S(1)} %add.231), channel_id=1, replica_groups=mesh['dp'=8,'expert'=4] {'expert'}, use_global_device_ids=true, to_apply=%region_20.21 | all-reduce | flops 1032 | bytes 8256 | tf_op jit(solution)/shard_map/psum | solution.py:225
  (182 shorter events, 37.7 us)
Async XLA Ops:
  7.2 96.9 %copy-start = (f32[256,4]{0,1:T(4,128)S(1)}, f32[256,4]{0,1:T(4,128)}, u32[]{:S(2)}) copy-start(f32[256,4]{0,1:T(4,128)} %param.23) | copy-start | bytes 12292
  7.2 27.9 %copy-start.3 = (f32[128,16]{0,1:T(8,128)S(1)}, f32[128,16]{0,1:T(8,128)}, u32[]{:S(2)}) copy-start(f32[128,16]{0,1:T(8,128)} %param.19) | copy-start | bytes 24580
  7.2 41.9 %copy-start.4 = (f32[128,16]{0,1:T(8,128)S(1)}, f32[128,16]{0,1:T(8,128)}, u32[]{:S(2)}) copy-start(f32[128,16]{0,1:T(8,128)} %param.20) | copy-start | bytes 24580
  7.2 85.9 %all-gather.14.cloned.1.call-start = ((), (), s32[]{:S(2)}) async-start(), calls=%async_computation.6 | async-start | bytes 1474560 | tf_op jit(solution)/shard_map/all_gather | solution.py:105
  8.2 41.2 %copy-start.12 = (f32[4]{0:T(128)S(1)}, f32[4]{0:T(128)}, u32[]{:S(2)}) copy-start(f32[4]{0:T(128)} %param.22) | copy-start | bytes 52
  34.0 16.2 %copy-start.1 = (bf16[128,256]{1,0:T(8,128)(2,1)S(1)}, bf16[128,256]{1,0:T(8,128)(2,1)}, u32[]{:S(2)}) copy-start(bf16[128,256]{1,0:T(8,128)(2,1)} %param.16) | copy-start | bytes 196612
  70.1 70.6 %reduce-scatter.3.cloned.1.call-start = ((), (), s32[]{:S(2)}) async-start(), calls=%async_computation.7 | async-start | bytes 1474560 | tf_op jit(solution)/shard_map/reduce_scatter | solution.py:109
  93.1 4.1 %copy-start.8 = (bf16[1,2048,896]{2,1,0:T(8,128)(2,1)S(1)}, bf16[1,2048,896]{2,1,0:T(8,128)(2,1)}, u32[]{:S(2)}) copy-start(bf16[1,2048,896]{2,1,0:T(8,128)(2,1)} %param.25) | copy-start | bytes 11010052
  93.1 4.1 %copy-start.11 = (bf16[320,2048]{1,0:T(8,128)(2,1)S(1)}, bf16[320,2048]{1,0:T(8,128)(2,1)}, u32[]{:S(2)}) copy-start(bf16[320,2048]{1,0:T(8,128)(2,1)} %all-gather.14.cloned.1.call-done) | copy-start | bytes 3932164
  97.2 2.6 copy-start.13
  97.2 3.4 %copy-start.7 = (bf16[1,896,2048]{2,1,0:T(8,128)(2,1)S(1)}, bf16[1,896,2048]{2,1,0:T(8,128)(2,1)}, u32[]{:S(2)}) copy-start(bf16[1,896,2048]{2,1,0:T(8,128)(2,1)} %param.26) | copy-start | bytes 11010052
  99.8 0.8 copy-start.14
  103.3 0.7 copy-start.6
  103.3 42.1 %copy-start.2 = (bf16[128,256]{1,0:T(8,128)(2,1)S(1)}, bf16[128,256]{1,0:T(8,128)(2,1)}, u32[]{:S(2)}) copy-start(bf16[128,256]{1,0:T(8,128)(2,1)} %param.27) | copy-start | bytes 196612
  140.7 13.6 %all-to-all-start.1 = ((bf16[4,80,256]{2,1,0:T(8,128)(2,1)}), bf16[4,80,256]{2,1,0:T(8,128)(2,1)S(1)}, u32[]{:S(2)}, u32[]{:S(2)}) async-start(bf16[4,80,256]{2,1,0:T(8,128)(2,1)} %bitcast.255), calls=%async_computation.2 | async-start | bytes 327680 | tf_op jit(solution)/shard_map/all_to_all | solution.py:113
  145.3 53.3 %all-gather.16.cloned.1.call-start = ((), (), s32[]{:S(2)}) async-start(), calls=%async_computation.8 | async-start | bytes 1474560 | tf_op jit(solution)/shard_map/all_gather | solution.py:105
  175.6 70.2 %reduce-scatter.5.cloned.1.call-start = ((), (), s32[]{:S(2)}) async-start(), calls=%async_computation.9 | async-start | bytes 1474560 | tf_op jit(solution)/shard_map/reduce_scatter | solution.py:109
  198.6 5.0 %copy-start.9 = (bf16[1,2048,896]{2,1,0:T(8,128)(2,1)S(1)}, bf16[1,2048,896]{2,1,0:T(8,128)(2,1)}, u32[]{:S(2)}) copy-start(bf16[1,2048,896]{2,1,0:T(8,128)(2,1)} %param.25) | copy-start | bytes 11010052
  203.6 1.6 copy-start.15
  203.6 2.2 copy-start.10
  210.2 5.5 %copy-start.16 = (bf16[320,896]{1,0:T(8,128)(2,1)S(1)}, bf16[320,896]{1,0:T(8,128)(2,1)}, u32[]{:S(2)}) copy-start(bf16[320,896]{1,0:T(8,128)(2,1)} %copy-done.15) | copy-start | bytes 1720324
  245.8 11.0 %all-to-all-start.3 = ((bf16[4,80,256]{2,1,0:T(8,128)(2,1)}), bf16[4,80,256]{2,1,0:T(8,128)(2,1)S(1)}, u32[]{:S(2)}, u32[]{:S(2)}) async-start(bf16[4,80,256]{2,1,0:T(8,128)(2,1)} %bitcast.254), calls=%async_computation.5 | async-start | bytes 327680 | tf_op jit(solution)/shard_map/all_to_all | solution.py:113
  283.6 4.1 %copy-start.5 = (f32[128,4]{0,1:T(4,128)S(1)}, f32[128,4]{0,1:T(4,128)}, u32[]{:S(2)}) copy-start(f32[128,4]{0,1:T(4,128)} %param.18) | copy-start | bytes 6148
Sparse Core Ops, SparseCore 0:
  70.2 22.8 all-gather.13
  103.5 37.1 reduce-scatter.2
  175.7 22.8 all-gather.15
  208.6 37.1 reduce-scatter.4
